TPU v7x, 32 devices: a whole 2x2x4 slice. The times are simulated.
32 devices in a mesh: img: 8 (over z, y), sp: 4 (over x, core).
Axes of the slice: x: 2, y: 2, z: 4, core: 2. Of those that a mesh axis runs over, the one named last changes fastest.
Arguments:
- patches: bfloat16 [4096, 1280], P(('img', 'sp')), parts along dimension 0, may hold values from -6 to 6
- pos_ids: int32 [2, 4096], P(None, 'img'), parts along dimension 1, may hold values from 0 to 31, as said below
- norm_gain: float32 [1280], replicated, may hold values from 0.5 to 1.5
- norm_bias: float32 [1280], replicated, may hold values from -3 to 3
- qkv_weight: bfloat16 [1280, 3, 1280], P(None, None, 'sp')
- qkv_bias: float32 [3, 1280], replicated, may hold values from -3 to 3
- proj_weight: bfloat16 [1280, 1280], P('sp'), may hold values from -0.15625 to 0.15625
- proj_bias: float32 [1280], replicated, may hold values from -3 to 3
- merge_gain: float32 [1280], replicated, may hold values from 0.5 to 1.5
- merge_bias: float32 [1280], replicated, may hold values from -3 to 3
- fc1_weight: bfloat16 [5120, 5120], P(None, 'sp'), may hold values from -0.078125 to 0.078125
- fc1_bias: float32 [5120], P('sp'), may hold values from -3 to 3
Outputs:
- vit_out: bfloat16 [4096, 1280], P(('img', 'sp')), parts along dimension 0
- merged_hidden: bfloat16 [1024, 5120], P('img', 'sp'), parts along dimension 0
There are 8 independent parts, one for each index of `img`. A program takes and returns all parts, laid end to end along the dimension named above; an argument that names none is the same for every part. Nothing has to cross between parts.
Inputs may be any that keep to these rules, and one draw needn't show every extreme that they name: pos_ids[0] and pos_ids[1] are the row and column of each patch on a grid of 2 R by 2 C patches, where the grid of 2x2 blocks has R rows and C columns, R C = 128, and one of R and C equals min(8, 128); each aligned run of 4 patches is one 2x2 block in row-major order inside it; every block of the grid appears once, in the order that the argument gives.
All inputs are finite; a program needn't handle non-finite values.
Results may differ from a plain program's by a relative error of at most 0.006.
Values may be sent and summed in bfloat16 or wider, within the bound.
No kernel may reach another device: no remote copies, remote signals or barrier semaphores. Data moves between devices by JAX's collectives and lax.ppermute only.
A program may use at most 64 MiB of HBM per device.

v0:
```python
import jax
import jax.numpy as jnp
from jax import lax
from jax.sharding import PartitionSpec as P

HEADS = 16


def layer_norm(values, gain, bias):
    mean = jnp.mean(values, axis=-1, keepdims=True)
    centered = values - mean
    var = jnp.mean(centered * centered, axis=-1, keepdims=True)
    return centered * lax.rsqrt(var + 1e-06) * gain + bias


def rotate(values, positions, nheads):
    count = values.shape[0]
    hdim = values.shape[1] // nheads
    quarter = hdim // 4
    inv = 1.0 / 10000.0 ** (jnp.arange(quarter, dtype=jnp.float32) * 2.0 / (hdim // 2))
    rows = positions[0].astype(jnp.float32)[:, None] * inv
    cols = positions[1].astype(jnp.float32)[:, None] * inv
    angle = jnp.concatenate([rows, cols, rows, cols], axis=1)
    cosine = jnp.cos(angle)[:, None, :]
    sine = jnp.sin(angle)[:, None, :]
    shaped = values.reshape(count, nheads, hdim)
    half = hdim // 2
    turned = jnp.concatenate([-shaped[..., half:], shaped[..., :half]], axis=-1)
    return (shaped * cosine + turned * sine).reshape(count, nheads * hdim)


def attend(query, keys, value, nheads, hdim):
    count = query.shape[0]
    block = min(512, count)
    qblocks = query.reshape(count // block, block, nheads, hdim)
    kshaped = keys.reshape(count, nheads, hdim)
    vshaped = value.reshape(count, nheads, hdim)
    scale = 1.0 / jnp.sqrt(jnp.float32(hdim))

    def one_block(qpart):
        scores = (
            jnp.einsum("bhd,khd->hbk", qpart, kshaped, preferred_element_type=jnp.float32) * scale
        )
        top = jnp.max(scores, axis=-1, keepdims=True)
        expo = jnp.exp(scores - top)
        weights = (expo / jnp.sum(expo, axis=-1, keepdims=True)).astype(jnp.bfloat16)
        result = jnp.einsum("hbk,khd->bhd", weights, vshaped, preferred_element_type=jnp.float32)
        return result.astype(jnp.bfloat16).reshape(block, nheads * hdim)

    return lax.map(one_block, qblocks).reshape(count, nheads * hdim)


def per_device(
    patches,
    pos_ids,
    norm_gain,
    norm_bias,
    qkv_weight,
    qkv_bias,
    proj_weight,
    proj_bias,
    merge_gain,
    merge_bias,
    fc1_weight,
    fc1_bias,
):
    groups = lax.axis_size("sp")
    where = lax.axis_index("sp")
    prow = patches.shape[0]
    width = patches.shape[1]
    heads_local = HEADS // groups
    hdim = width // HEADS
    local_width = width // groups
    xfloat = patches.astype(jnp.float32)
    normed = layer_norm(xfloat, norm_gain, norm_bias).astype(jnp.bfloat16)
    bias_local = lax.dynamic_slice_in_dim(qkv_bias, where * local_width, local_width, 1)
    qkv = (
        jnp.einsum(
            "pd,dcn->pcn",
            lax.all_gather(normed, "sp", axis=0, tiled=True),
            qkv_weight,
            preferred_element_type=jnp.float32,
        )
        + bias_local[None]
    )
    query = rotate(qkv[:, 0], pos_ids, heads_local).astype(jnp.bfloat16)
    keys = rotate(qkv[:, 1], pos_ids, heads_local).astype(jnp.bfloat16)
    value = qkv[:, 2].astype(jnp.bfloat16)
    spread = jnp.stack([query, keys, value])
    attended = attend(spread[0], spread[1], spread[2], heads_local, hdim)
    returned = lax.all_to_all(attended, "sp", split_axis=0, concat_axis=1, tiled=True)
    projected = jnp.dot(
        returned,
        lax.all_gather(proj_weight, "sp", axis=0, tiled=True),
        preferred_element_type=jnp.float32,
    )
    vit_out = (xfloat + projected + proj_bias).astype(jnp.bfloat16)
    zn = layer_norm(vit_out.astype(jnp.float32), merge_gain, merge_bias).astype(jnp.bfloat16)
    blocks = zn.reshape(prow // 4, 4 * width)
    hidden = (
        jnp.dot(
            lax.all_gather(blocks, "sp", axis=0, tiled=True),
            fc1_weight,
            preferred_element_type=jnp.float32,
        )
        + fc1_bias
    )
    merged_hidden = jax.nn.gelu(hidden, approximate=False).astype(jnp.bfloat16)
    return (vit_out, merged_hidden)


def solution(mesh):
    return jax.shard_map(
        per_device,
        mesh=mesh,
        in_specs=(
            P(("img", "sp"), None),
            P(None, "img"),
            P(),
            P(),
            P(None, None, "sp"),
            P(),
            P("sp", None),
            P(),
            P(),
            P(),
            P(None, "sp"),
            P("sp"),
        ),
        out_specs=(P(("img", "sp"), None), P("img", "sp")),
        check_vma=False,
    )
```

profile of v0, /device:TPU:0, one launch (start us, length us, event | category | flops | bytes accessed | tf_op | source)
XLA Modules:
  0.0 105.2 jit_solution(13298240738997939612)
XLA Ops:
  7.2 1.2 %convert_reduce_fusion = f32[128]{0:T(128)S(1)} fusion(bf16[128,1280]{1,0:T(8,128)(2,1)} %param.12), kind=kLoop, calls=%fused_computation.17 | loop fusion | flops 327552 | bytes 328192 | tf_op jit(solution)/shard_map/reduce_sum | solution.py:10
  8.5 1.2 %fusion.15 = f32[128]{0:T(128)S(1)} fusion(bf16[128,1280]{1,0:T(8,128)(2,1)} %param.12, f32[128]{0:T(128)S(1)} %broadcast_multiply_fusion.3), kind=kLoop, calls=%fused_computation.24 | loop fusion | flops 655232 | bytes 328704 | tf_op jit(solution)/shard_map/reduce_sum | solution.py:12
  9.7 2.0 %fusion.18 = bf16[128,1280]{1,0:T(8,128)(2,1)} fusion(bf16[128,1280]{1,0:T(8,128)(2,1)} %param.12, f32[1280]{0:T(1024)} %param.15, f32[1280]{0:T(1024)} %param.14, f32[128]{0:T(128)S(1)} %add_rsqrt_fusion.1, f32[128]{0:T(128)S(1)} %broadcast_multiply_fusion.3), kind=kLoop, calls=%fused_computation.27 | loop fusion | flops 983040 | bytes 666624 | tf_op jit(solution)/shard_map/convert_element_type | solution.py:75
  11.8 0.7 all-gather.6.cloned.1.call-update
  12.5 0.8 constant_dynamic-slice_fusion
  13.3 0.8 slice_convert_fusion.2
  14.2 0.6 fusion.40
  14.7 18.0 %all-gather.4.cloned.1.call-done = bf16[512,1280]{1,0:T(8,128)(2,1)} async-done(((bf16[128,1280]{1,0:T(8,128)(2,1)}), bf16[512,1280]{1,0:T(8,128)(2,1)}) %all-gather.4.cloned.1.call-update) | async-done | bytes 1310736 | tf_op jit(solution)/shard_map/all_gather | solution.py:80
  32.8 2.8 %convolution_add_fusion.2 = f32[512,3,320]{0,2,1:T(8,128)S(1)} fusion(bf16[1280,3,320]{0,2,1:T(8,128)(2,1)S(1)} %copy-done, bf16[512,1280]{1,0:T(8,128)(2,1)} %all-gather.4.cloned.1.call-done, f32[3,320]{1,0:T(4,128)S(1)} %constant_dynamic-slice_fusion), kind=kOutput, calls=%fused_computation.11 | convolution fusion | flops 1258782720 | bytes 5738240 | tf_op jit(solution)/shard_map/pd,dcn->pcn/dot_general | solution.py:78
  35.5 0.8 slice.51
  36.3 0.1 fusion.42
  36.4 0.1 slice_negate_fusion
  36.6 0.4 fusion.29
  37.0 3.4 %fusion.43 = (f32[4,512]{1,0:T(4,128)S(1)}, f32[4,512,512]{1,2,0:T(8,128)}) fusion(bf16[512,4,80]{0,2,1:T(8,128)(2,1)S(1)} %get-tuple-element.24, bf16[512,4,80]{0,2,1:T(8,128)(2,1)S(1)} %get-tuple-element.23), kind=kOutput, calls=%fused_computation.75 | convolution fusion | flops 170918400 | bytes 4857856 | tf_op jit(solution)/shard_map/while/body/eval_jaxpr/sub | solution.py:45
  40.4 3.1 %fusion.10 = bf16[512,4,80]{0,2,1:T(8,128)(2,1)S(1)} fusion(bf16[512,4,80]{0,2,1:T(8,128)(2,1)S(1)} %bitcast.30, f32[4,512,512]{1,2,0:T(8,128)} %get-tuple-element.32, f32[4,512]{1,0:T(4,128)S(1)} %get-tuple-element.31), kind=kOutput, calls=%fused_computation.14 | convolution fusion | flops 170033152 | bytes 4857856 | tf_op jit(solution)/shard_map/while/body/eval_jaxpr/hbk,khd->bhd/dot_general | solution.py:47
  43.5 0.1 all_to_all.14
  43.6 13.0 %all_to_all.19 = bf16[4,128,320]{1,2,0:T(8,128)(2,1)S(1)} all-to-all(bf16[4,128,320]{1,2,0:T(8,128)(2,1)S(1)} %copy.16), channel_id=1, replica_groups=mesh['img'=8,'sp'=4] {'sp'}, dimensions={0} | all-to-all | bytes 655360 | tf_op jit(solution)/shard_map/all_to_all | solution.py:91
  56.6 10.5 %all-gather.6.cloned.1.call-done = bf16[1280,1280]{1,0:T(8,128)(2,1)} async-done(((bf16[320,1280]{1,0:T(8,128)(2,1)}), bf16[1280,1280]{1,0:T(8,128)(2,1)}) %all-gather.6.cloned.1.call-update) | async-done | bytes 3276816 | tf_op jit(solution)/shard_map/all_gather | solution.py:94
  67.1 2.7 %convert_reduce_fusion.1 = (f32[128]{0:T(128)S(1)}, bf16[128,1280]{1,0:T(8,128)(2,1)S(1)}) fusion(f32[1280]{0:T(1024)S(1)} %copy-done.4, bf16[128,1280]{0,1:T(8,128)(2,1)S(1)} %bitcast.29, bf16[1280,1280]{1,0:T(8,128)(2,1)} %all-gather.6.cloned.1.call-done, bf16[128,1280]{1,0:T(8,128)(2,1)S(1)} %copy-done.1), kind=kOutput, calls=%fused_computation.19 | convolution fusion | flops 420413312 | bytes 4265472 | tf_op jit(solution)/shard_map/dot_general | solution.py:92
  69.8 0.2 fusion.19
  70.1 0.3 fusion.22
  70.4 0.9 reshape.180
  71.3 18.3 %all-gather.8.cloned.1.call-done = bf16[128,5120]{1,0:T(8,128)(2,1)} async-done(((bf16[32,5120]{1,0:T(8,128)(2,1)}), bf16[128,5120]{1,0:T(8,128)(2,1)}) %all-gather.8.cloned.1.call-update) | async-done | bytes 1310736 | tf_op jit(solution)/shard_map/all_gather | solution.py:102
  89.6 9.1 %fusion.25 = bf16[128,1280]{1,0:T(8,128)(2,1)} fusion(bf16[128,5120]{1,0:T(8,128)(2,1)} %all-gather.8.cloned.1.call-done, bf16[5120,1280]{1,0:T(8,128)(2,1)} %param.22, f32[1280]{0:T(1024)S(1)} %copy-done.7), kind=kOutput, calls=%fused_computation.34 | convolution fusion | flops 1688535040 | bytes 14750720 | tf_op jit(solution)/shard_map/dot_general | solution.py:101
  (28 shorter events, 0.4 us)
Async XLA Ops:
  7.2 25.6 %copy-start = (bf16[1280,3,320]{0,2,1:T(8,128)(2,1)S(1)}, bf16[1280,3,320]{0,2,1:T(8,128)(2,1)}, u32[]{:S(2)}) copy-start(bf16[1280,3,320]{0,2,1:T(8,128)(2,1)} %param.16) | copy-start | bytes 7372804
  7.2 25.6 %all-gather.4.cloned.1.call-start = ((), (), s32[]{:S(2)}) async-start(), calls=%async_computation.1 | async-start | bytes 1638400 | tf_op jit(solution)/shard_map/all_gather | solution.py:80
  11.7 55.4 %all-gather.6.cloned.1.call-start = ((), (), s32[]{:S(2)}) async-start(), calls=%async_computation.2 | async-start | bytes 4096000 | tf_op jit(solution)/shard_map/all_gather | solution.py:94
  12.5 77.2 %all-gather.8.cloned.1.call-start = ((), (), s32[]{:S(2)}) async-start(), calls=%async_computation.3 | async-start | bytes 1638400 | tf_op jit(solution)/shard_map/all_gather | solution.py:102
  36.9 3.5 %copy-start.3 = (bf16[512,1,320]{0,2,1:T(8,128)(2,1)S(1)}, bf16[512,1,320]{0,2,1:T(8,128)(2,1)}, u32[]{:S(2)}) copy-start(bf16[512,1,320]{0,2,1:T(8,128)(2,1)} %slice.51) | copy-start | bytes 983044
  40.4 26.7 %copy-start.1 = (bf16[128,1280]{1,0:T(8,128)(2,1)S(1)}, bf16[128,1280]{1,0:T(8,128)(2,1)}, u32[]{:S(2)}) copy-start(bf16[128,1280]{1,0:T(8,128)(2,1)} %param.12) | copy-start | bytes 983044
  40.4 26.7 %copy-start.4 = (f32[1280]{0:T(1024)S(1)}, f32[1280]{0:T(1024)}, u32[]{:S(2)}) copy-start(f32[1280]{0:T(1024)} %param.19) | copy-start | bytes 15364
  43.5 26.6 %copy-start.5 = (f32[1280]{0:T(1024)S(1)}, f32[1280]{0:T(1024)}, u32[]{:S(2)}) copy-start(f32[1280]{0:T(1024)} %param.21) | copy-start | bytes 15364
  43.5 26.6 %copy-start.6 = (f32[1280]{0:T(1024)S(1)}, f32[1280]{0:T(1024)}, u32[]{:S(2)}) copy-start(f32[1280]{0:T(1024)} %param.20) | copy-start | bytes 15364
  56.6 33.0 %copy-start.7 = (f32[1280]{0:T(1024)S(1)}, f32[1280]{0:T(1024)}, u32[]{:S(2)}) copy-start(f32[1280]{0:T(1024)} %param.23) | copy-start | bytes 15364
  69.8 28.9 %copy-start.2 = (bf16[128,1280]{1,0:T(8,128)(2,1)}, bf16[128,1280]{1,0:T(8,128)(2,1)S(1)}, u32[]{:S(2)}) copy-start(bf16[128,1280]{1,0:T(8,128)(2,1)S(1)} %get-tuple-element.34) | copy-start | bytes 983044
Sparse Core Ops, SparseCore 0:
  11.8 20.8 all-gather.3
  34.3 32.7 all-gather.5
  71.4 18.1 all-gather.7
where the time goes:
time: 106 us; the launch traced here: 105 us
  waiting for transfers between devices  47.5 us (45%)
  matrix products  21 us (20%)
  between operations  13.9 us (13%)
  blocking collectives  13 us (12%)
  other arithmetic  6.95 us (7%)
  local copies, waits for them, and re-layouts  2.74 us (3%)
    all_gather x1, waiting for transfers between devices, per_device(): lax.all_gather(blocks, 'sp', axis=0, tiled=True)  18.3 us
    all_gather x1, waiting for transfers between devices, per_device(): lax.all_gather(normed, 'sp', axis=0, tiled=True)  18 us
    all_to_all x1, blocking collectives, per_device(): lax.all_to_all(attended, 'sp', split_axis=0, concat_axis=1, tiled=True)  13 us
    all_gather x1, waiting for transfers between devices, per_device(): lax.all_gather(proj_weight, 'sp', axis=0, tiled=True)  10.5 us
    dot_general x1, matrix products, per_device(): jnp.dot(lax.all_gather(blocks, 'sp', axis=0, tiled=True), fc1_weight, pre...  9.06 us
    sub x1, matrix products, one_block(): expo = jnp.exp(scores - top)  3.44 us
    dot_general x1, matrix products, one_block(): jnp.einsum('hbk,khd->bhd', weights, vshaped, preferred_element_type=jnp.f...  3.07 us
    dot_general x1, matrix products, per_device(): jnp.einsum('pd,dcn->pcn', lax.all_gather(normed, 'sp', axis=0, tiled=True...  2.77 us
  transfers between devices with their start and end apart: 3, of which 3 were waited for; matrix products, arithmetic and copies ran while one was open for 12% of the time, Pallas kernels for 0%

commit v1 on v0

--- a/solution.py
+++ b/solution.py
@@ -4,6 +4,13 @@
 from jax.sharding import PartitionSpec as P
 
 HEADS = 16
+
+
+def attach_the_links(state, dim_no):
+    plain = list(state.shape[1:])
+    plain[dim_no] *= state.shape[0]
+    f_next = jnp.moveaxis(state, 0, dim_no).reshape(plain)
+    return f_next
 
 
 def layer_norm(values, gain, bias):
@@ -74,12 +81,37 @@
     xfloat = patches.astype(jnp.float32)
     normed = layer_norm(xfloat, norm_gain, norm_bias).astype(jnp.bfloat16)
     bias_local = lax.dynamic_slice_in_dim(qkv_bias, where * local_width, local_width, 1)
+
+    def rates_supply(view, along_axis, dim_k, mine_x, on_dim):
+        cards = []
+        v_now, next_value, local_out = (
+            lax.axis_size(along_axis),
+            lax.axis_index(along_axis),
+            view.shape[dim_k],
+        )
+        for w in range(v_now):
+            cards.append((w, (w + 1) % v_now))
+        bank = []
+        answer = view
+        for i0 in range(v_now):
+            row_out = answer if i0 == v_now - 1 else lax.ppermute(answer, along_axis, cards)
+            left_arr = mine_x(answer, (next_value - i0) % v_now * local_out)
+            bank.append(left_arr)
+            answer = row_out
+        r_now = jnp.stack(bank)
+        bank = r_now[(next_value - jnp.arange(v_now)) % v_now]
+        small = attach_the_links(bank, on_dim)
+        return small
+
     qkv = (
-        jnp.einsum(
-            "pd,dcn->pcn",
-            lax.all_gather(normed, "sp", axis=0, tiled=True),
-            qkv_weight,
-            preferred_element_type=jnp.float32,
+        rates_supply(
+            normed,
+            "sp",
+            0,
+            lambda shard, offset: jnp.einsum(
+                "pd,dcn->pcn", shard, qkv_weight, preferred_element_type=jnp.float32
+            ),
+            0,
         )
         + bias_local[None]
     )

time: 106 us -> 110 us (1.038)
  local copies, waits for them, and re-layouts: 2.74 us -> 6.25 us
  blocking collectives: 13 us -> 10.6 us
  other arithmetic: 6.95 us -> 9.28 us
  starting transfers between devices: 0.12 us -> 2.02 us
  waiting for transfers between devices: 47.5 us -> 46.1 us
    ppermute x0 -> x3, waiting for transfers between devices: none -> 26.3 us  [rates_supply(): lax.ppermute(answer, along_axis, cards)]
    all_gather x1 -> x0, waiting for transfers between devices: 18 us -> none  [per_device(): lax.all_gather(normed, 'sp', axis=0, tiled=True)]
    all_gather x1, waiting for transfers between devices: 10.5 us -> 0.01 us  [per_device(): lax.all_gather(proj_weight, 'sp', axis=0, tiled=True)]
    gather x0 -> x1, local copies, waits for them, and re-layouts: none -> 3.51 us  [rates_supply(): bank = r_now[(next_value - jnp.arange(v_now)) % v_now]]
    all_to_all x1, blocking collectives: 13 us -> 10.6 us  [per_device(): lax.all_to_all(attended, 'sp', split_axis=0, concat_axis=1, tiled=True)]
    ppermute x0 -> x3, starting transfers between devices: none -> 1.94 us  [rates_supply(): lax.ppermute(answer, along_axis, cards)]
    add x0 -> x1, other arithmetic: none -> 1.74 us  [per_device(): rates_supply(normed, 'sp', 0, lambda shard, offset: jnp.einsum('pd,dcn->p...]
    another operation x0 -> x1, other arithmetic: none -> 1.46 us  [rates_supply(): r_now = jnp.stack(bank)]
  transfers between devices with their start and end apart: 3 -> 5, of which waited for: 3 -> 4; matrix products, arithmetic and copies ran while one was open for 12% -> 21% of each run, Pallas kernels for 0% -> 0%
where the time goes in v1:
time: 110 us
  waiting for transfers between devices  46.1 us (42%)
  matrix products  21.1 us (19%)
  between operations  14.2 us (13%)
  blocking collectives  10.6 us (10%)
  other arithmetic  9.28 us (8%)
  local copies, waits for them, and re-layouts  6.25 us (6%)
  starting transfers between devices  2.02 us (2%)
    ppermute x3, waiting for transfers between devices, rates_supply(): lax.ppermute(answer, along_axis, cards)  26.3 us
    all_gather x1, waiting for transfers between devices, per_device(): lax.all_gather(blocks, 'sp', axis=0, tiled=True)  19.1 us
    all_to_all x1, blocking collectives, per_device(): lax.all_to_all(attended, 'sp', split_axis=0, concat_axis=1, tiled=True)  10.6 us
    dot_general x1, matrix products, per_device(): jnp.dot(lax.all_gather(blocks, 'sp', axis=0, tiled=True), fc1_weight, pre...  9.06 us
    gather x1, local copies, waits for them, and re-layouts, rates_supply(): bank = r_now[(next_value - jnp.arange(v_now)) % v_now]  3.51 us
    sub x1, matrix products, one_block(): expo = jnp.exp(scores - top)  3.44 us
    dot_general x4, matrix products, per_device(): jnp.einsum('pd,dcn->pcn', shard, qkv_weight, preferred_element_type=jnp.f...  3.18 us
    dot_general x1, matrix products, one_block(): jnp.einsum('hbk,khd->bhd', weights, vshaped, preferred_element_type=jnp.f...  2.73 us
  transfers between devices with their start and end apart: 5, of which 4 were waited for; matrix products, arithmetic and copies ran while one was open for 21% of the time, Pallas kernels for 0%

profile of v1, /device:TPU:0, one launch (start us, length us, event | category | flops | bytes accessed | tf_op | source)
XLA Modules:
  0.0 109.6 jit_solution(10923002193124021199)
XLA Ops:
  8.0 1.1 %convert_reduce_fusion = f32[128]{0:T(128)S(1)} fusion(bf16[128,1280]{1,0:T(8,128)(2,1)} %param.12), kind=kLoop, calls=%fused_computation.22 | loop fusion | flops 327552 | bytes 328192 | tf_op jit(solution)/shard_map/reduce_sum | solution.py:17
  9.1 1.2 %fusion.14 = f32[128]{0:T(128)S(1)} fusion(bf16[128,1280]{1,0:T(8,128)(2,1)} %param.12, f32[128]{0:T(128)S(1)} %broadcast_multiply_fusion.3), kind=kLoop, calls=%fused_computation.29 | loop fusion | flops 655232 | bytes 328704 | tf_op jit(solution)/shard_map/reduce_sum | solution.py:19
  10.3 1.3 %fusion.17 = bf16[128,1280]{1,0:T(8,128)(2,1)S(1)} fusion(bf16[128,1280]{1,0:T(8,128)(2,1)} %param.12, f32[1280]{0:T(1024)} %param.15, f32[1280]{0:T(1024)} %param.14, f32[128]{0:T(128)S(1)} %add_rsqrt_fusion.1, f32[128]{0:T(128)S(1)} %broadcast_multiply_fusion.3), kind=kLoop, calls=%fused_computation.32 | loop fusion | flops 983040 | bytes 666624 | tf_op jit(solution)/shard_map/convert_element_type | solution.py:82
  12.1 0.8 constant_dynamic-slice_fusion
  12.9 0.8 slice_convert_fusion.2
  14.3 4.4 %collective-permute-done = bf16[128,1280]{1,0:T(8,128)(2,1)S(1)} collective-permute-done((bf16[128,1280]{1,0:T(8,128)(2,1)S(1)}, bf16[128,1280]{1,0:T(8,128)(2,1)S(1)}, u32[]{:S(2)}, u32[]{:S(2)}) %collective-permute-start) | collective-permute-done | bytes 327712 | tf_op jit(solution)/shard_map/ppermute | solution.py:97
  18.8 0.8 convolution_bitcast_fusion.3
  19.6 11.2 %collective-permute-done.1 = bf16[128,1280]{1,0:T(8,128)(2,1)S(1)} collective-permute-done((bf16[128,1280]{1,0:T(8,128)(2,1)S(1)}, bf16[128,1280]{1,0:T(8,128)(2,1)S(1)}, u32[]{:S(2)}, u32[]{:S(2)}) %collective-permute-start.1) | collective-permute-done | bytes 327712 | tf_op jit(solution)/shard_map/ppermute | solution.py:97
  30.8 1.4 %collective-permute-start.2 = (bf16[128,1280]{1,0:T(8,128)(2,1)S(1)}, bf16[128,1280]{1,0:T(8,128)(2,1)S(1)}, u32[]{:S(2)}, u32[]{:S(2)}) collective-permute-start(bf16[128,1280]{1,0:T(8,128)(2,1)S(1)} %collective-permute-done.1), channel_id=1, source_target_pairs={{0,1},{1,2},{2,3},{3,0},{4,5},{5,6},{6,7},{7,4},{8,9},{9,10},{10,1... | collective-permute-start | bytes 983048 | tf_op jit(solution)/shard_map/ppermute | solution.py:97
  32.2 0.8 convolution_bitcast_fusion.2
  33.0 0.8 convolution_bitcast_fusion.1
  33.8 10.7 %collective-permute-done.2 = bf16[128,1280]{1,0:T(8,128)(2,1)S(1)} collective-permute-done((bf16[128,1280]{1,0:T(8,128)(2,1)S(1)}, bf16[128,1280]{1,0:T(8,128)(2,1)S(1)}, u32[]{:S(2)}, u32[]{:S(2)}) %collective-permute-start.2) | collective-permute-done | bytes 327712 | tf_op jit(solution)/shard_map/ppermute | solution.py:97
  44.5 0.8 convolution_bitcast_fusion
  45.3 1.5 %pad_maximum_fusion = f32[4,128,3,320]{1,3,2,0:T(8,128)} fusion(f32[1,128,3,320]{1,3,2,0:T(8,128)S(1)} %convolution_bitcast_fusion, f32[1,128,3,320]{1,3,2,0:T(8,128)S(1)} %convolution_bitcast_fusion.1, f32[1,128,3,320]{1,3,2,0:T(8,128)S(1)} %convolution_bitcast_fusion.2, f32[1,128,3,320]{1,3,2,0:T(8,128)S(1)} %convolution_bitcast_fusion.3), kind=kLoop, calls=%fused_computation.13 | loop fusion | flops 1474560 | bytes 3932160 | tf_op jit(solution)/shard_map/stack | solution.py:101
  46.7 3.5 %gather_fusion = f32[4,128,3,320]{1,3,2,0:T(8,128)} fusion(f32[4,128,3,320]{1,3,2,0:T(8,128)} %pad_maximum_fusion, s32[1024]{0:T(1024)S(1)} %pad_clamp_fusion), kind=kCustom, calls=%fused_computation | custom fusion | bytes 3932176 | tf_op jit(solution)/shard_map/gather | solution.py:102
  50.2 1.7 %bitcast_add_fusion = f32[512,3,320]{0,2,1:T(8,128)S(1)} fusion(f32[3,320]{1,0:T(4,128)S(1)} %constant_dynamic-slice_fusion, f32[4,128,3,320]{1,3,2,0:T(8,128)} %gather_fusion), kind=kLoop, calls=%fused_computation.12 | loop fusion | flops 491520 | bytes 3936000 | tf_op jit(solution)/shard_map/add | solution.py:107
  52.0 0.8 slice.53
  53.4 3.4 %fusion.48 = (f32[4,512]{1,0:T(4,128)S(1)}, f32[4,512,512]{1,2,0:T(8,128)}) fusion(bf16[512,4,80]{0,2,1:T(8,128)(2,1)S(1)} %get-tuple-element.24, bf16[512,4,80]{0,2,1:T(8,128)(2,1)S(1)} %get-tuple-element.23), kind=kOutput, calls=%fused_computation.91 | convolution fusion | flops 170918400 | bytes 4857856 | tf_op jit(solution)/shard_map/while/body/eval_jaxpr/sub | solution.py:52
  56.9 2.7 %fusion.9 = bf16[512,4,80]{0,2,1:T(8,128)(2,1)S(1)} fusion(bf16[512,4,80]{0,2,1:T(8,128)(2,1)S(1)} %bitcast.57, f32[4,512,512]{1,2,0:T(8,128)} %get-tuple-element.32, f32[4,512]{1,0:T(4,128)S(1)} %get-tuple-element.31), kind=kOutput, calls=%fused_computation.19 | convolution fusion | flops 170033152 | bytes 4857856 | tf_op jit(solution)/shard_map/while/body/eval_jaxpr/hbk,khd->bhd/dot_general | solution.py:54
  59.7 10.6 %all_to_all.19 = bf16[4,128,320]{1,2,0:T(8,128)(2,1)S(1)} all-to-all(bf16[4,128,320]{1,2,0:T(8,128)(2,1)S(1)} %copy.17), channel_id=1, replica_groups=mesh['img'=8,'sp'=4] {'sp'}, dimensions={0} | all-to-all | bytes 655360 | tf_op jit(solution)/shard_map/all_to_all | solution.py:123
  70.4 2.7 %convert_reduce_fusion.1 = (f32[128]{0:T(128)S(1)}, bf16[128,1280]{1,0:T(8,128)(2,1)S(1)}) fusion(f32[1280]{0:T(1024)S(1)} %copy-done.4, bf16[128,1280]{0,1:T(8,128)(2,1)S(1)} %bitcast.56, bf16[1280,1280]{1,0:T(8,128)(2,1)} %all-gather.3.cloned.1.call-done, bf16[128,1280]{1,0:T(8,128)(2,1)S(1)} %copy-done.1), kind=kOutput, calls=%fused_computation.24 | convolution fusion | flops 420413312 | bytes 4265472 | tf_op jit(solution)/shard_map/dot_general | solution.py:124
  73.6 0.9 reshape.233
  74.6 19.1 %all-gather.5.cloned.1.call-done = bf16[128,5120]{1,0:T(8,128)(2,1)} async-done(((bf16[32,5120]{1,0:T(8,128)(2,1)}), bf16[128,5120]{1,0:T(8,128)(2,1)}) %all-gather.5.cloned.1.call-update) | async-done | bytes 1310736 | tf_op jit(solution)/shard_map/all_gather | solution.py:134
  93.7 9.1 %fusion.24 = bf16[128,1280]{1,0:T(8,128)(2,1)} fusion(bf16[128,5120]{1,0:T(8,128)(2,1)} %all-gather.5.cloned.1.call-done, bf16[5120,1280]{1,0:T(8,128)(2,1)} %param.22, f32[1280]{0:T(1024)S(1)} %copy-done.7), kind=kOutput, calls=%fused_computation.39 | convolution fusion | flops 1688535040 | bytes 14750720 | tf_op jit(solution)/shard_map/dot_general | solution.py:133
  (39 shorter events, 3.3 us)
Async XLA Ops:
  7.2 11.6 %copy-start = (bf16[1280,3,320]{0,2,1:T(8,128)(2,1)S(1)}, bf16[1280,3,320]{0,2,1:T(8,128)(2,1)}, u32[]{:S(2)}) copy-start(bf16[1280,3,320]{0,2,1:T(8,128)(2,1)} %param.16) | copy-start | bytes 7372804
  7.2 63.2 %all-gather.3.cloned.1.call-start = ((), (), s32[]{:S(2)}) async-start(), calls=%async_computation.1 | async-start | bytes 4096000 | tf_op jit(solution)/shard_map/all_gather | solution.py:126
  7.9 85.8 %all-gather.5.cloned.1.call-start = ((), (), s32[]{:S(2)}) async-start(), calls=%async_computation.2 | async-start | bytes 1638400 | tf_op jit(solution)/shard_map/all_gather | solution.py:134
  11.6 7.2 %collective-permute-start = (bf16[128,1280]{1,0:T(8,128)(2,1)S(1)}, bf16[128,1280]{1,0:T(8,128)(2,1)S(1)}, u32[]{:S(2)}, u32[]{:S(2)}) collective-permute-start(bf16[128,1280]{1,0:T(8,128)(2,1)S(1)} %fusion.17), channel_id=1, source_target_pairs={{0,1},{1,2},{2,3},{3,0},{4,5},{5,6},{6,7},{7,4},{8,9},{9,10},{10,1... | collective-permute-start | bytes 983048 | tf_op jit(solution)/shard_map/ppermute | solution.py:97
  18.8 12.1 %collective-permute-start.1 = (bf16[128,1280]{1,0:T(8,128)(2,1)S(1)}, bf16[128,1280]{1,0:T(8,128)(2,1)S(1)}, u32[]{:S(2)}, u32[]{:S(2)}) collective-permute-start(bf16[128,1280]{1,0:T(8,128)(2,1)S(1)} %collective-permute-done), channel_id=1, source_target_pairs={{0,1},{1,2},{2,3},{3,0},{4,5},{5,6},{6,7},{7,4},{8,9},{9,10},{10,1... | collective-permute-start | bytes 983048 | tf_op jit(solution)/shard_map/ppermute | solution.py:97
  30.8 13.6 %collective-permute-start.2 = (bf16[128,1280]{1,0:T(8,128)(2,1)S(1)}, bf16[128,1280]{1,0:T(8,128)(2,1)S(1)}, u32[]{:S(2)}, u32[]{:S(2)}) collective-permute-start(bf16[128,1280]{1,0:T(8,128)(2,1)S(1)} %collective-permute-done.1), channel_id=1, source_target_pairs={{0,1},{1,2},{2,3},{3,0},{4,5},{5,6},{6,7},{7,4},{8,9},{9,10},{10,1... | collective-permute-start | bytes 983048 | tf_op jit(solution)/shard_map/ppermute | solution.py:97
  53.4 3.5 %copy-start.3 = (bf16[512,1,320]{0,2,1:T(8,128)(2,1)S(1)}, bf16[512,1,320]{0,2,1:T(8,128)(2,1)}, u32[]{:S(2)}) copy-start(bf16[512,1,320]{0,2,1:T(8,128)(2,1)} %slice.53) | copy-start | bytes 983044
  56.8 13.5 %copy-start.1 = (bf16[128,1280]{1,0:T(8,128)(2,1)S(1)}, bf16[128,1280]{1,0:T(8,128)(2,1)}, u32[]{:S(2)}) copy-start(bf16[128,1280]{1,0:T(8,128)(2,1)} %param.12) | copy-start | bytes 983044
  56.8 13.5 %copy-start.4 = (f32[1280]{0:T(1024)S(1)}, f32[1280]{0:T(1024)}, u32[]{:S(2)}) copy-start(f32[1280]{0:T(1024)} %param.19) | copy-start | bytes 15364
  70.3 3.0 %copy-start.5 = (f32[1280]{0:T(1024)S(1)}, f32[1280]{0:T(1024)}, u32[]{:S(2)}) copy-start(f32[1280]{0:T(1024)} %param.21) | copy-start | bytes 15364
  70.4 3.0 %copy-start.6 = (f32[1280]{0:T(1024)S(1)}, f32[1280]{0:T(1024)}, u32[]{:S(2)}) copy-start(f32[1280]{0:T(1024)} %param.20) | copy-start | bytes 15364
  70.4 23.3 %copy-start.7 = (f32[1280]{0:T(1024)S(1)}, f32[1280]{0:T(1024)}, u32[]{:S(2)}) copy-start(f32[1280]{0:T(1024)} %param.23) | copy-start | bytes 15364
  73.1 29.7 %copy-start.2 = (bf16[128,1280]{1,0:T(8,128)(2,1)}, bf16[128,1280]{1,0:T(8,128)(2,1)S(1)}, u32[]{:S(2)}) copy-start(bf16[128,1280]{1,0:T(8,128)(2,1)S(1)} %get-tuple-element.34) | copy-start | bytes 983044
Sparse Core Ops, SparseCore 0:
  9.5 38.3 all-gather.2
  74.7 18.9 all-gather.4
